TPU v7x, 32 devices: a whole 2x2x4 slice. The times are simulated.
32 devices in a mesh: dp: 4 (over y, x), tensor: 2 (over core), precond: 4 (over z).
Axes of the slice: x: 2, y: 2, z: 4, core: 2. Of those that a mesh axis runs over, the one named last changes fastest.
Arguments:
- tokens: bfloat16 [512, 8192], P('dp', 'tensor'), may hold values from -6 to 6
- gain: bfloat16 [8192], P('tensor'), may hold values from 0.099609375 to 1.8984375
- cotangent: bfloat16 [512, 12288], P('dp', 'precond'), may hold values from -6 to 6
Outputs:
- preconditioner: float32 [8, 1024, 1024], P('tensor', ('dp', 'precond'))
All inputs are finite; a program needn't handle non-finite values.
Results may differ from a plain program's by a relative error of at most 0.00089.
Values sent between devices are 32-bit elements; how exact they have to be, the bound alone decides.
No kernel may reach another device: no remote copies, remote signals or barrier semaphores. Data moves between devices by JAX's collectives and lax.ppermute only.
A program may use at most 128 MiB of HBM per device.

v0:
```python
import jax
import jax.numpy as jnp
from jax import lax
from jax.sharding import PartitionSpec as P

BLK = 1024
highest = lax.Precision.HIGHEST
epsilon = 1e-06
damping = 0.01


def batched(left_side, right_side):
    return jnp.einsum("bij,bjk->bik", left_side, right_side, precision=highest)


def body(tokens, gain, cotangent):
    values = tokens.astype(jnp.float32)
    square_part = jnp.sum(values * values, axis=1)[None, :]
    gathered = lax.all_gather(square_part, "tensor", axis=0, tiled=True)
    mean_square = jnp.sum(gathered, axis=0)[:, None] / (values.shape[1] * lax.axis_size("tensor"))
    normed = (values * lax.rsqrt(mean_square + epsilon) * gain.astype(jnp.float32)).astype(
        jnp.bfloat16
    )
    token_total = tokens.shape[0] * lax.axis_size("dp")
    partial_value = lax.dot_general(
        normed, cotangent, (((0,), (0,)), ((), ())), preferred_element_type=jnp.float32
    )
    gradient = lax.psum_scatter(partial_value, "dp", scatter_dimension=1, tiled=True) / token_total
    block_count = gradient.shape[0] // BLK
    blocks = gradient.reshape(block_count, BLK, gradient.shape[1])
    local_gram = jnp.einsum("bik,bjk->bij", blocks, blocks, precision=highest)
    identity = jnp.eye(BLK, dtype=jnp.float32)
    summed_gram = lax.psum(local_gram, ("dp", "precond"))
    statistic = summed_gram + damping * identity
    scaling = 2.0 * jnp.trace(statistic, axis1=1, axis2=2)[:, None, None] / BLK
    start_iterate = statistic / scaling
    factor_one = (5.0 * identity - start_iterate) / 4.0
    row_count = BLK // (lax.axis_size("dp") * lax.axis_size("precond"))
    offset = (
        lax.axis_index("dp") * lax.axis_size("precond") + lax.axis_index("precond")
    ) * row_count
    factor_rows = lax.dynamic_slice_in_dim(factor_one, offset, row_count, 1)
    power_two = batched(factor_rows, factor_one)
    power_three = batched(power_two, factor_one)
    power_four = batched(power_three, factor_one)
    power_five = batched(power_four, factor_one)
    product = batched(power_five, start_iterate)
    return jnp.power(scaling, -0.25) * (5.0 * factor_rows - product) / 4.0


def solution(mesh):
    in_specs = (P("dp", "tensor"), P("tensor"), P("dp", "precond"))
    out_specs = P("tensor", ("dp", "precond"), None)
    return jax.shard_map(body, mesh=mesh, in_specs=in_specs, out_specs=out_specs, check_vma=False)
```

profile of v0, /device:TPU:0, one launch (start us, length us, event | category | flops | bytes accessed | tf_op | source)
XLA Modules:
  0.0 1049.3 jit_solution(3601064974182051058)
XLA Ops:
  6.5 0.0 copy-start
  6.5 0.0 reduce-scatter.2.cloned.1.call-start
  6.5 0.8 convert_element_type.11
  7.3 1.5 fusion.2
  8.8 2.0 all-gather.1
  10.8 0.0 copy-done
  10.8 20.7 %fusion.7 = f32[4096,3072]{1,0:T(8,128)} fusion(bf16[128,3072]{1,0:T(8,128)(2,1)S(1)} %copy-done, bf16[128,4096]{1,0:T(8,128)(2,1)} %param.3, f32[4096]{0:T(1024)S(1)} %convert_element_type.11, f32[128]{0:T(128)S(1)} %add_rsqrt_fusion), kind=kOutput, calls=%fused_computation.15 | convolution fusion | flops 3223322624 | bytes 52183552 | tf_op jit(solution)/shard_map/dot_general | solution.py:25
  31.5 0.0 reduce-scatter.2.cloned.1.call-update
  31.6 0.0 all-reduce.2.cloned.1.call-start
  31.6 426.7 %reduce-scatter.2.cloned.1.call-done = f32[4096,768]{1,0:T(8,128)} async-done(((f32[4096,3072]{1,0:T(8,128)}), f32[4096,768]{1,0:T(8,128)}) %reduce-scatter.2.cloned.1.call-update) | async-done | bytes 12582928 | tf_op jit(solution)/shard_map/reduce_scatter | solution.py:28
  458.3 10.0 broadcast_multiply_fusion
  468.2 47.3 %fusion.14 = f32[4,1024,1024]{2,1,0:T(8,128)} fusion(f32[4,1024,768]{2,1,0:T(8,128)} %bitcast.13), kind=kOutput, calls=%fused_computation.24 | convolution fusion | flops 38654705664 | bytes 29360128 | tf_op jit(solution)/shard_map/bik,bjk->bij/dot_general | solution.py:31
  515.5 0.0 all-reduce.2.cloned.1.call-update
  515.6 0.3 iota_compare_fusion
  515.9 4.3 fusion
  520.2 446.5 %all-reduce.2.cloned.1.call-done = f32[4,1024,1024]{2,1,0:T(8,128)} async-done(((f32[4,1024,1024]{2,1,0:T(8,128)}), f32[4,1024,1024]{2,1,0:T(8,128)}) %all-reduce.2.cloned.1.call-update) | async-done | bytes 16777232 | tf_op jit(solution)/shard_map/psum | solution.py:33
  966.8 0.0 copy-start.2
  966.8 0.0 copy-start.3
  966.8 10.3 select_reduce_fusion
  977.0 0.0 copy-done.2
  977.0 0.0 copy-done.3
  977.0 8.1 subtract_multiply_fusion
  985.2 10.2 fusion.11
  995.4 10.4 fusion.15
  1005.8 10.4 fusion.16
  1016.2 10.3 fusion.17
  1026.5 0.0 copy-start.1
  1026.5 15.7 %fusion.6 = f32[4,64,1024]{2,1,0:T(8,128)} fusion(f32[4,64,1024]{2,1,0:T(8,128)S(1)} %fusion.17, f32[4,1024,1024]{2,1,0:T(8,128)S(1)} %subtract_multiply_fusion, s32[]{:T(128)S(6)} %select_n.9, f32[4]{0:T(128)S(1)} %get-tuple-element.5, f32[4,1024,1024]{2,1,0:T(8,128)} %all-reduce.2.cloned.1.call-done, f32[4]{0:T(128)S(1)} %get-tuple-element.6, ...), kind=kOutput, calls=%fused_computation.14 | convolution fusion | flops 3230662656 | bytes 24117284 | tf_op jit(solution)/shard_map/bij,bjk->bik/dot_general | solution.py:13
  1042.2 0.0 copy-done.1
  (3 shorter events, 0.0 us)
Async XLA Ops:
  6.5 4.3 copy-start
  6.5 451.7 %reduce-scatter.2.cloned.1.call-start = ((), (), s32[]{:S(2)}) async-start(), calls=%async_computation.1 | async-start | bytes 62914560 | tf_op jit(solution)/shard_map/reduce_scatter | solution.py:28
  31.6 935.2 %all-reduce.2.cloned.1.call-start = ((), (), s32[]{:S(2)}) async-start(), calls=%async_computation.2 | async-start | bytes 33554432 | tf_op jit(solution)/shard_map/psum | solution.py:33
  966.8 10.3 copy-start.2
  966.8 10.3 copy-start.3
  1026.5 15.7 %copy-start.1 = (bf16[128,3072]{1,0:T(8,128)(2,1)S(1)}, bf16[128,3072]{1,0:T(8,128)(2,1)}, u32[]{:S(2)}) copy-start(bf16[128,3072]{1,0:T(8,128)(2,1)} %param.5) | copy-start | bytes 2359300
Sparse Core Ops, SparseCore 0:
  31.7 426.5 reduce-scatter.1
  515.7 451.0 all-reduce.1
where the time goes:
time: 1050 us
  waiting for transfers between devices  873 us (83%)
  matrix products  125 us (12%)
  other arithmetic  35.3 us (3%)
  between operations  13.8 us (1%)
    psum x1, waiting for transfers between devices, body(): summed_gram = lax.psum(local_gram, ('dp', 'precond'))  447 us
    reduce_scatter x1, waiting for transfers between devices, body(): lax.psum_scatter(partial_value, 'dp', scatter_dimension=1, tiled=True)  427 us
    dot_general x5, matrix products, batched(): return jnp.einsum('bij,bjk->bik', left_side, right_side, precision=highest)  57 us
    dot_general x1, matrix products, body(): local_gram = jnp.einsum('bik,bjk->bij', blocks, blocks, precision=highest)  47.3 us
  transfers between devices with their start and end apart: 2, of which 2 were waited for; matrix products, arithmetic and copies ran while one was open for 0% of the time, Pallas kernels for 0%

commit v1 on v0

--- a/solution.py
+++ b/solution.py
@@ -2,6 +2,7 @@
 import jax.numpy as jnp
 from jax import lax
 from jax.sharding import PartitionSpec as P
+from jax.lax import psum
 
 BLK = 1024
 highest = lax.Precision.HIGHEST
@@ -30,7 +31,8 @@
     blocks = gradient.reshape(block_count, BLK, gradient.shape[1])
     local_gram = jnp.einsum("bik,bjk->bij", blocks, blocks, precision=highest)
     identity = jnp.eye(BLK, dtype=jnp.float32)
-    summed_gram = lax.psum(local_gram, ("dp", "precond"))
+    loops_solve = lambda s0, mesh_ax, a_name: psum(psum(s0, mesh_ax), a_name)
+    summed_gram = loops_solve(local_gram, "precond", "dp")
     statistic = summed_gram + damping * identity
     scaling = 2.0 * jnp.trace(statistic, axis1=1, axis2=2)[:, None, None] / BLK
     start_iterate = statistic / scaling

time: 1050 us -> 1470 us (1.40)
  waiting for transfers between devices: 873 us -> 1290 us
    psum x1 -> x2, waiting for transfers between devices: 447 us -> 867 us  [body(): loops_solve = lambda s0, mesh_ax, a_name: psum(psum(s0, mesh_ax), a_name)]
  transfers between devices with their start and end apart: 2 -> 3, of which waited for: 2 -> 3; matrix products, arithmetic and copies ran while one was open for 0% -> 0% of each run, Pallas kernels for 0% -> 0%
where the time goes in v1:
time: 1470 us
  waiting for transfers between devices  1290 us (88%)
  matrix products  125 us (9%)
  other arithmetic  35.3 us (2%)
    psum x2, waiting for transfers between devices, body(): loops_solve = lambda s0, mesh_ax, a_name: psum(psum(s0, mesh_ax), a_name)  867 us
    reduce_scatter x1, waiting for transfers between devices, body(): lax.psum_scatter(partial_value, 'dp', scatter_dimension=1, tiled=True)  426 us
    dot_general x5, matrix products, batched(): return jnp.einsum('bij,bjk->bik', left_side, right_side, precision=highest)  57 us
    dot_general x1, matrix products, body(): local_gram = jnp.einsum('bik,bjk->bij', blocks, blocks, precision=highest)  47.2 us
  transfers between devices with their start and end apart: 3, of which 3 were waited for; matrix products, arithmetic and copies ran while one was open for 0% of the time, Pallas kernels for 0%

profile of v1, /device:TPU:0, one launch (start us, length us, event | category | flops | bytes accessed | tf_op | source)
XLA Modules:
  0.0 1469.8 jit_solution(11345556893335817440)
XLA Ops:
  6.5 0.0 copy-start
  6.5 0.0 reduce-scatter.2.cloned.1.call-start
  6.5 0.8 convert_element_type.11
  7.3 1.5 fusion.2
  8.8 2.0 all-gather.1
  10.8 0.0 copy-done
  10.8 20.7 %fusion.7 = f32[4096,3072]{1,0:T(8,128)} fusion(bf16[128,3072]{1,0:T(8,128)(2,1)S(1)} %copy-done, bf16[128,4096]{1,0:T(8,128)(2,1)} %param.3, f32[4096]{0:T(1024)S(1)} %convert_element_type.11, f32[128]{0:T(128)S(1)} %add_rsqrt_fusion), kind=kOutput, calls=%fused_computation.15 | convolution fusion | flops 3223322624 | bytes 52183552 | tf_op jit(solution)/shard_map/dot_general | solution.py:26
  31.5 0.0 reduce-scatter.2.cloned.1.call-update
  31.6 0.2 all-reduce.3.cloned.1.call-start
  31.8 426.5 %reduce-scatter.2.cloned.1.call-done = f32[4096,768]{1,0:T(8,128)} async-done(((f32[4096,3072]{1,0:T(8,128)}), f32[4096,768]{1,0:T(8,128)}) %reduce-scatter.2.cloned.1.call-update) | async-done | bytes 12582928 | tf_op jit(solution)/shard_map/reduce_scatter | solution.py:29
  458.3 10.0 broadcast_multiply_fusion
  468.2 47.2 %fusion.14 = f32[4,1024,1024]{2,1,0:T(8,128)} fusion(f32[4,1024,768]{2,1,0:T(8,128)} %bitcast.13), kind=kOutput, calls=%fused_computation.24 | convolution fusion | flops 38654705664 | bytes 29360128 | tf_op jit(solution)/shard_map/bik,bjk->bij/dot_general | solution.py:32
  515.4 0.0 all-reduce.3.cloned.1.call-update
  515.4 0.0 all-reduce.5.cloned.1.call-start
  515.5 562.3 %all-reduce.3.cloned.1.call-done = f32[4,1024,1024]{2,1,0:T(8,128)} async-done(((f32[4,1024,1024]{2,1,0:T(8,128)}), f32[4,1024,1024]{2,1,0:T(8,128)}) %all-reduce.3.cloned.1.call-update) | async-done | bytes 16777232 | tf_op jit(solution)/shard_map/psum | solution.py:34
  1077.7 0.0 all-reduce.5.cloned.1.call-update
  1077.7 0.3 iota_compare_fusion
  1078.1 4.3 fusion
  1082.4 305.2 %all-reduce.5.cloned.1.call-done = f32[4,1024,1024]{2,1,0:T(8,128)} async-done(((f32[4,1024,1024]{2,1,0:T(8,128)}), f32[4,1024,1024]{2,1,0:T(8,128)}) %all-reduce.5.cloned.1.call-update) | async-done | bytes 16777232 | tf_op jit(solution)/shard_map/psum | solution.py:34
  1387.6 0.0 copy-start.2
  1387.6 0.0 copy-start.3
  1387.6 10.3 select_reduce_fusion
  1397.9 0.0 copy-done.2
  1397.9 0.0 copy-done.3
  1397.9 8.1 subtract_multiply_fusion
  1406.0 10.2 fusion.11
  1416.2 10.4 fusion.15
  1426.6 10.4 fusion.16
  1437.1 10.3 fusion.17
  1447.3 0.0 copy-start.1
  1447.3 15.7 %fusion.6 = f32[4,64,1024]{2,1,0:T(8,128)} fusion(f32[4,64,1024]{2,1,0:T(8,128)S(1)} %fusion.17, f32[4,1024,1024]{2,1,0:T(8,128)S(1)} %subtract_multiply_fusion, s32[]{:T(128)S(6)} %select_n.9, f32[4]{0:T(128)S(1)} %get-tuple-element.5, f32[4,1024,1024]{2,1,0:T(8,128)} %all-reduce.5.cloned.1.call-done, f32[4]{0:T(128)S(1)} %get-tuple-element.6, ...), kind=kOutput, calls=%fused_computation.14 | convolution fusion | flops 3230662656 | bytes 24117284 | tf_op jit(solution)/shard_map/bij,bjk->bik/dot_general | solution.py:14
  1463.0 0.0 copy-done.1
  (3 shorter events, 0.0 us)
Async XLA Ops:
  6.5 4.3 copy-start
  6.5 451.7 %reduce-scatter.2.cloned.1.call-start = ((), (), s32[]{:S(2)}) async-start(), calls=%async_computation.1 | async-start | bytes 62914560 | tf_op jit(solution)/shard_map/reduce_scatter | solution.py:29
  31.6 1046.2 %all-reduce.3.cloned.1.call-start = ((), (), s32[]{:S(2)}) async-start(), calls=%async_computation.2 | async-start | bytes 33554432 | tf_op jit(solution)/shard_map/psum | solution.py:34
  515.4 872.2 %all-reduce.5.cloned.1.call-start = ((), (), s32[]{:S(2)}) async-start(), calls=%async_computation.3 | async-start | bytes 33554432 | tf_op jit(solution)/shard_map/psum | solution.py:34
  1387.6 10.3 copy-start.2
  1387.6 10.3 copy-start.3
  1447.3 15.7 %copy-start.1 = (bf16[128,3072]{1,0:T(8,128)(2,1)S(1)}, bf16[128,3072]{1,0:T(8,128)(2,1)}, u32[]{:S(2)}) copy-start(bf16[128,3072]{1,0:T(8,128)(2,1)} %param.5) | copy-start | bytes 2359300
Sparse Core Ops, SparseCore 0:
  31.7 426.5 reduce-scatter.1
  515.5 562.1 all-reduce.2
  1081.3 306.2 all-reduce.4
